TPU v7x, 512 devices: a 8x2x16 block of a 8x16x16 slice. The times are simulated.
512 devices in a mesh: ckpt: 2 (over y), row: 32 (over z, core), col: 8 (over x).
Axes of the slice: x: 8, y: 2, z: 16, core: 2. Of those that a mesh axis runs over, the one named last changes fastest.
The devices are a block of a 8x16x16 slice.
Arguments:
- grad_slab: bfloat16 [768, 27648], P(('ckpt', 'col'), 'row'), parts along dimension 0, may hold values from -6 to 6
- eigenbasis: bfloat16 [55296, 14336], P(('ckpt', 'row'), 'col'), parts along dimension 0, may hold values from -0.0625 to 0.0625
- eigenvalues: bfloat16 [768, 14336], P('ckpt', 'col'), parts along dimension 0, may hold values from 0.049804688 to 5
Outputs:
- preconditioned: bfloat16 [768, 27648], P(('ckpt', 'col'), 'row'), parts along dimension 0
There are 2 independent parts, one for each index of `ckpt`. A program takes and returns all parts, laid end to end along the dimension named above; each array names one. Nothing has to cross between parts.
All inputs are finite; a program needn't handle non-finite values.
Results may differ from a plain program's by a relative error of at most 0.0046.
Values may be sent and summed in bfloat16 or wider, within the bound.
A program may use at most 64 MiB of HBM per device.

v0:
```python
import jax
import jax.numpy as jnp
from jax import lax
from jax.sharding import Mesh
from jax.sharding import PartitionSpec as P

ROW = ("row_0", "row_1")
CKPT_ROW = ("ckpt", "row_0", "row_1")


DAMPING = 0.1


def laid_out(blocks, dim):
    blocks = jnp.moveaxis(blocks, 0, dim)
    lengths = blocks.shape
    return blocks.reshape(*lengths[:dim], lengths[dim] * lengths[dim + 1], *lengths[dim + 2 :])


def copy_for_each(value, axis):
    copies = jnp.broadcast_to(value, (lax.axis_size(axis), *value.shape))
    return lax.all_to_all(copies, axis, split_axis=0, concat_axis=0, tiled=True)


def gather_directly(value, axis, dim):
    return laid_out(copy_for_each(value, axis), dim)


def reduced_to_own(blocks, axes, order):
    inside = blocks.shape[1:]
    blocks = blocks.reshape(*(lax.axis_size(a) for a in axes), *inside)
    blocks = jnp.moveaxis(blocks, order, range(len(axes))).reshape(-1, *inside)
    for k in order:
        blocks = lax.psum_scatter(blocks, axes[k], scatter_dimension=0, tiled=True)
    return blocks[0]


def split_up(value, dim, count):
    before, after = (value.shape[:dim], value.shape[dim + 1 :])
    return jnp.moveaxis(value.reshape(*before, count, -1, *after), dim, 0)


def scatter_axes(value, axes, order, dim):
    count = lax.axis_size(axes)
    return reduced_to_own(split_up(value, dim, count), axes, order)


def all_blocks(value, axes, order):
    blocks = value[None]
    for k in order:
        blocks = lax.all_gather(blocks, axes[k], axis=0, tiled=True)
    carried = [lax.axis_size(axes[k]) for k in reversed(order)]
    blocks = blocks.reshape(*carried, *value.shape)
    turned = sorted(range(len(order)), key=lambda place: order[len(order) - 1 - place])
    return blocks.transpose(*turned, *range(len(order), blocks.ndim)).reshape(-1, *value.shape)


def whole_of(value, axes, order, dim):
    return laid_out(all_blocks(value, axes, order), dim)


def summed_on_arrival(value, axis, dim):
    count = lax.axis_size(axis)
    blocks = lax.all_to_all(split_up(value, dim, count), axis, 0, 0, tiled=True)
    return jnp.sum(blocks, axis=0)


def on_device(grad_slab, eigenbasis, eigenvalues):
    rotated_part = jnp.dot(
        gather_directly(grad_slab, "col", 0), eigenbasis, preferred_element_type=jnp.float32
    )
    own_share = scatter_axes(rotated_part, ROW, (1, 0), 1)
    share_width = own_share.shape[1]
    offset = lax.axis_index(ROW) * share_width
    own_values = lax.dynamic_slice_in_dim(eigenvalues, offset, share_width, 1)
    scaled_share = (own_share / (own_values.astype(jnp.float32) + DAMPING)).astype(jnp.bfloat16)
    scaled = whole_of(scaled_share, ROW, (0, 1), 1)
    result = summed_on_arrival(
        lax.dot_general(
            scaled, eigenbasis, (((1,), (1,)), ((), ())), preferred_element_type=jnp.float32
        ),
        "col",
        0,
    )
    return result.astype(jnp.bfloat16)


def solution(mesh):
    torus = Mesh(
        mesh.devices.reshape(mesh.shape["ckpt"], 16, 2, mesh.shape["col"]),
        ("ckpt", "row_0", "row_1", "col"),
    )
    return jax.shard_map(
        on_device,
        mesh=torus,
        in_specs=(P(("ckpt", "col"), ROW), P(CKPT_ROW, "col"), P("ckpt", "col")),
        out_specs=P(("ckpt", "col"), ROW),
        check_vma=False,
    )
```

profile of v0, /device:TPU:80, one launch (start us, length us, event | category | flops | bytes accessed | tf_op | source)
XLA Modules:
  0.0 312.7 jit_solution(3465347139622952609)
XLA Ops:
  6.5 1.8 broadcast_in_dim.6
  8.3 7.3 %all-to-all-start = ((bf16[8,48,864]{2,1,0:T(8,128)(2,1)}), bf16[8,48,864]{2,1,0:T(8,128)(2,1)}, u32[]{:S(2)}, u32[]{:S(2)}) async-start(bf16[8,48,864]{2,1,0:T(8,128)(2,1)} %broadcast_in_dim.6), calls=%async_computation | async-start | bytes 1376256 | tf_op jit(solution)/shard_map/all_to_all | solution.py:22
  15.7 0.1 reduce-scatter.3.cloned.1.call-start
  15.7 4.5 %copy.16 = bf16[864,1792]{0,1:T(8,128)(2,1)S(1)} copy(bf16[864,1792]{1,0:T(8,128)(2,1)} %param.4) | data formatting | bytes 6193152 | tf_op args[1]
  20.3 16.6 %all-to-all-done = bf16[8,48,864]{2,1,0:T(8,128)(2,1)} async-done(((bf16[8,48,864]{2,1,0:T(8,128)(2,1)}), bf16[8,48,864]{2,1,0:T(8,128)(2,1)}, u32[]{:S(2)}, u32[]{:S(2)}) %all-to-all-start) | async-done | bytes 663584 | tf_op jit(solution)/shard_map/all_to_all | solution.py:22
  36.8 4.8 %fusion.3 = f32[384,32,56]{0,2,1:T(8,128)} fusion(bf16[384,864,1]{1,0,2:T(8,128)(2,1)} %bitcast.1, bf16[32,56,864]{2,1,0:T(8,128)(2,1)S(1)} %bitcast.32), kind=kOutput, calls=%fused_computation.4 | convolution fusion | flops 1189085184 | bytes 6512640 | tf_op jit(solution)/shard_map/dot_general | solution.py:69
  41.6 5.6 %copy.18 = f32[2,16,384,56]{3,2,1,0:T(8,128)} copy(f32[2,16,384,56]{2,3,0,1:T(8,128)} %bitcast.33) | data formatting | bytes 5505024 | tf_op jit(solution)/shard_map/transpose | solution.py:32
  47.3 0.1 reduce-scatter.3.cloned.1.call-update
  47.3 0.1 reduce-scatter.5.cloned.1.call-start
  47.4 54.1 %reduce-scatter.3.cloned.1.call-done = f32[16,384,56]{2,1,0:T(8,128)} async-done(((f32[32,384,56]{2,1,0:T(8,128)}), f32[16,384,56]{2,1,0:T(8,128)}) %reduce-scatter.3.cloned.1.call-update) | async-done | bytes 1376272 | tf_op jit(solution)/shard_map/reduce_scatter | solution.py:34
  101.5 0.1 reduce-scatter.5.cloned.1.call-update
  101.6 0.1 all-gather.3.cloned.1.call-start
  101.6 83.9 %reduce-scatter.5.cloned.1.call-done = f32[1,384,56]{2,1,0:T(8,128)} async-done(((f32[16,384,56]{2,1,0:T(8,128)}), f32[1,384,56]{2,1,0:T(8,128)}) %reduce-scatter.5.cloned.1.call-update) | async-done | bytes 86032 | tf_op jit(solution)/shard_map/reduce_scatter | solution.py:34
  185.6 1.1 fusion.2
  186.7 38.4 %all-gather = bf16[6144,56]{1,0:T(8,128)(2,1)S(1)} all-gather(bf16[384,56]{1,0:T(8,128)(2,1)S(1)} %fusion.2), channel_id=2, replica_groups=mesh['ckpt'=2,'row_0'=16,'row_1'=2,'col'=8] {'row_0'}, dimensions={0}, use_global_device_ids=true | all-gather | bytes 731136 | tf_op jit(solution)/shard_map/all_gather | solution.py:51
  225.1 1.4 copy.20
  226.5 0.1 all-gather.3.cloned.1.call-update
  226.5 18.8 %all-gather.3.cloned.1.call-done = bf16[32,384,56]{1,2,0:T(8,128)(2,1)} async-done(((bf16[16,384,56]{1,2,0:T(8,128)(2,1)}), bf16[32,384,56]{1,2,0:T(8,128)(2,1)}) %all-gather.3.cloned.1.call-update) | async-done | bytes 1376272 | tf_op jit(solution)/shard_map/all_gather | solution.py:51
  245.3 7.0 %copy.21 = bf16[16,2,384,56]{3,1,0,2:T(2,128)(2,1)S(1)} copy(bf16[16,2,384,56]{2,3,0,1:T(8,128)(2,1)} %bitcast.34) | data formatting | bytes 2752512 | tf_op jit(solution)/shard_map/transpose | solution.py:55
  252.3 6.5 %dot_general.15 = bf16[8,48,1792]{2,1,0:T(8,128)(2,1)} reshape(bf16[384,32,56]{2,1,0:T(8,128)(2,1)S(1)} %bitcast.30) | data formatting | bytes 2752512 | tf_op jit(solution)/shard_map/dot_general | solution.py:79
  258.8 3.9 %fusion = f32[8,48,864]{2,1,0:T(8,128)S(1)} fusion(bf16[8,48,1792]{2,1,0:T(8,128)(2,1)} %dot_general.15, bf16[864,1792]{1,0:T(8,128)(2,1)} %param.4), kind=kOutput, calls=%fused_computation | convolution fusion | flops 1189085184 | bytes 5799936 | tf_op jit(solution)/shard_map/dot_general | solution.py:79
  262.7 42.7 %all_to_all.10 = f32[8,48,864]{2,1,0:T(8,128)S(1)} all-to-all(f32[8,48,864]{2,1,0:T(8,128)S(1)} %fusion), channel_id=1, replica_groups=mesh['ckpt'=2,'row_0'=16,'row_1'=2,'col'=8] {'col'}, dimensions={0} | all-to-all | bytes 2654208 | tf_op jit(solution)/shard_map/all_to_all | solution.py:64
  305.4 0.7 reduce_sum.9
Async XLA Ops:
  8.3 28.5 %all-to-all-start = ((bf16[8,48,864]{2,1,0:T(8,128)(2,1)}), bf16[8,48,864]{2,1,0:T(8,128)(2,1)}, u32[]{:S(2)}, u32[]{:S(2)}) async-start(bf16[8,48,864]{2,1,0:T(8,128)(2,1)} %broadcast_in_dim.6), calls=%async_computation | async-start | bytes 1376256 | tf_op jit(solution)/shard_map/all_to_all | solution.py:22
  15.7 85.8 %reduce-scatter.3.cloned.1.call-start = ((), (), s32[]{:S(2)}) async-start(), calls=%async_computation.4 | async-start | bytes 9437184 | tf_op jit(solution)/shard_map/reduce_scatter | solution.py:34
  47.3 138.2 %reduce-scatter.5.cloned.1.call-start = ((), (), s32[]{:S(2)}) async-start(), calls=%async_computation.5 | async-start | bytes 3342336 | tf_op jit(solution)/shard_map/reduce_scatter | solution.py:34
  101.6 143.7 %all-gather.3.cloned.1.call-start = ((), (), s32[]{:S(2)}) async-start(), calls=%async_computation.6 | async-start | bytes 2064384 | tf_op jit(solution)/shard_map/all_gather | solution.py:51
Sparse Core Ops, SparseCore 0:
  47.4 54.0 reduce-scatter.2
  104.4 81.1 reduce-scatter.4
  226.6 18.5 all-gather.2
where the time goes:
time: 315 us; the launch traced here: 313 us
  waiting for transfers between devices  174 us (55%)
  blocking collectives  81.1 us (26%)
  local copies, waits for them, and re-layouts  26.9 us (9%)
  between operations  13.2 us (4%)
  matrix products  8.71 us (3%)
  starting transfers between devices  7.5 us (2%)
    reduce_scatter x2, waiting for transfers between devices, reduced_to_own(): blocks = lax.psum_scatter(blocks, axes[k], scatter_dimension=0, tiled=True)  138 us
    all_to_all x1, blocking collectives, summed_on_arrival(): blocks = lax.all_to_all(split_up(value, dim, count), axis, 0, 0, tiled=True)  42.7 us
    all_gather x1, blocking collectives, all_blocks(): blocks = lax.all_gather(blocks, axes[k], axis=0, tiled=True)  38.4 us
    all_gather x1, waiting for transfers between devices, all_blocks(): blocks = lax.all_gather(blocks, axes[k], axis=0, tiled=True)  18.8 us
    all_to_all x1, waiting for transfers between devices, copy_for_each(): return lax.all_to_all(copies, axis, split_axis=0, concat_axis=0, tiled=True)  16.6 us
    all_to_all x1, starting transfers between devices, copy_for_each(): return lax.all_to_all(copies, axis, split_axis=0, concat_axis=0, tiled=True)  7.32 us
    transpose x1, local copies, waits for them, and re-layouts, all_blocks(): blocks.transpose(*turned, *range(len(order), blocks.ndim))  7 us
    dot_general x1, local copies, waits for them, and re-layouts, on_device(): lax.dot_general(scaled, eigenbasis, (((1,), (1,)), ((), ())), preferred_e...  6.53 us
  transfers between devices with their start and end apart: 4, of which 4 were waited for; matrix products, arithmetic and copies ran while one was open for 1% of the time, Pallas kernels for 0%

commit v1 on v0

v1 whole, which is shorter than its diff:
```python
import functools

import jax
import jax.numpy as jnp
from jax import lax
from jax.experimental import pallas as pl
from jax.experimental.pallas import tpu as pltpu
from jax.sharding import PartitionSpec as P

DAMPING = 0.1
MESH = pl.DeviceIdType.MESH
CORES = 2
CHUNKS = 3
NZ = 16
NX = 8
BF16 = jnp.bfloat16
F32 = jnp.float32
N_SEMS = 48


class Labels:
    def __init__(self):
        self.index = {}

    def __call__(self, k, *label):
        return self.index.setdefault((k, *label), len(self.index))


def kernel(
    grad, eig, values, out,
    e_v, g_all, ev, psend, precv, acc,
    b1s, b1r, b2s, b2r, b3s, b3r, sc, res, d1s, d1r, d2s, d2r,
    local_sem, send_sem, recv_sem,
):
    r = lax.axis_index("row")
    x = lax.axis_index("col")
    z, c = lax.div(r, CORES), lax.rem(r, CORES)
    other = 1 - c
    unit_rows, half = acc.shape[2], acc.shape[3]
    h = g_all.shape[2]
    sem = Labels()
    started = []

    def copy(src, dst, index, row, col):
        return pltpu.make_async_remote_copy(
            src_ref=src, dst_ref=dst, send_sem=send_sem.at[index], recv_sem=recv_sem.at[index],
            device_id={"row": row, "col": col}, device_id_type=MESH,
        )

    def send(src, dst, index, row, col):
        c_ = copy(src, dst, index, row, col)
        c_.start()
        started.append(c_)

    def arrived(dst, index):
        copy(dst, dst, index, CORES * z + other, x).wait_recv()

    def zrow(offset):
        return lax.rem(z + (offset + NZ), NZ) * CORES + c

    def zunit(offset):
        return lax.rem(z + (offset + NZ), NZ)

    def xcol(offset):
        return lax.rem(x + (offset + NX), NX)

    loads = []
    own_g = []
    for k in range(CHUNKS):
        own_g.append(pltpu.make_async_copy(
            grad.at[pl.ds(k * h, h)], g_all.at[k, x], local_sem.at[1 + k]))
        own_g[-1].start()
    load_e = pltpu.make_async_copy(eig, e_v, local_sem.at[0])
    load_e.start()
    block = lax.div(z, 2)
    for k in range(CHUNKS):
        first = block * (CHUNKS * h) + k * h + lax.rem(z, 2) * unit_rows
        loads.append(pltpu.make_async_copy(
            values.at[pl.ds(pl.multiple_of(first, unit_rows), unit_rows),
                      pl.ds(pl.multiple_of(c * half, 128), half)],
            ev.at[k], local_sem.at[1 + CHUNKS + k]))
        loads[-1].start()

    barrier = pltpu.get_barrier_semaphore()
    partners = [(CORES * z + other, x)]
    partners += [(zrow(o), x) for o in (1, -1, 2, -2, 5, -5)]
    partners += [(r, xcol(o)) for o in (1, -1, 3, -3)]
    for row, col in partners:
        pl.semaphore_signal(barrier, inc=1, device_id={"row": row, "col": col}, device_id_type=MESH)
    pl.semaphore_wait(barrier, len(partners))

    def steps_of(k):
        s = -1 if k % 2 else 1
        zz_row = lambda o: zrow(s * o)
        zz = lambda o: zunit(s * o)
        xx = lambda o: xcol(s * o)
        own_cols = pl.ds(pl.multiple_of(c * half, 128), half)
        other_cols = pl.ds(pl.multiple_of(other * half, 128), half)
        peer = CORES * z + other

        def a_send(block_at, label, to):
            send(g_all.at[k, block_at], g_all.at[k, block_at], sem(k, *label), r, to)

        def a_wait(block_at, label):
            arrived(g_all.at[k, block_at], sem(k, *label))

        def a0():
            own_g[k].wait()
            a_send(x, ("ad", 1), xx(1))
            a_send(x, ("ae", 1), xx(-1))

        def a_round(n):
            def step():
                a_wait(xx(-n), ("ad", n))
                if n < 4:
                    a_send(xx(-n), ("ad", n + 1), xx(1))
                    a_wait(xx(n), ("ae", n))
                    if n < 3:
                        a_send(xx(n), ("ae", n + 1), xx(-1))
            return step

        def m1():
            if k == 0:
                load_e.wait()
            g = g_all[k].reshape(NX * h, g_all.shape[3])
            p = jnp.dot(g, e_v[:, other_cols], preferred_element_type=F32)
            psend[k] = p.astype(BF16).reshape(psend.shape[1:])
            send(psend.at[k], precv.at[k], sem(k, "x"), peer, x)
            p = jnp.dot(g, e_v[:, own_cols], preferred_element_type=F32)
            acc[k] = p.reshape(acc.shape[1:])
            arrived(precv.at[k], sem(k, "x"))
            acc[k] = acc[k] + precv[k].astype(F32)
            for slot, d in enumerate((4, 8, 2, 6)):
                b1s[k, slot] = acc[k, zz(-d)].astype(BF16)
            for slot, e in enumerate((4, 2, 6)):
                b1s[k, 4 + slot] = acc[k, zz(e)].astype(BF16)
            for name, lo, n, to in (("b1a", 0, 2, -1), ("b1b", 4, 1, 1), ("b1c", 2, 2, -1), ("b1d", 5, 2, 1)):
                send(b1s.at[k, pl.ds(lo, n)], b1r.at[k, pl.ds(lo, n)], sem(k, name), zz_row(to), x)

        def l2():
            arrived(b1r.at[k, pl.ds(0, 2)], sem(k, "b1a"))
            arrived(b1r.at[k, pl.ds(4, 1)], sem(k, "b1b"))
            for slot, d in enumerate((3, 7)):
                b2s[k, slot] = (acc[k, zz(-d)] + b1r[k, slot].astype(F32)).astype(BF16)
            b2s[k, 2] = (acc[k, zz(3)] + b1r[k, 4].astype(F32)).astype(BF16)
            b2s[k, 3] = acc[k, zz(7)].astype(BF16)
            for name, lo, to in (("b2a", 0, -2), ("b2b", 2, 2)):
                send(b2s.at[k, pl.ds(lo, 2)], b2r.at[k, pl.ds(lo, 2)], sem(k, name), zz_row(to), x)

        def l3():
            arrived(b1r.at[k, pl.ds(2, 2)], sem(k, "b1c"))
            arrived(b1r.at[k, pl.ds(5, 2)], sem(k, "b1d"))
            arrived(b2r.at[k, pl.ds(0, 2)], sem(k, "b2a"))
            arrived(b2r.at[k, pl.ds(2, 2)], sem(k, "b2b"))
            for slot, o, one, two in ((1, -5, 3, 1), (3, 5, 6, 3), (0, -1, 2, 0), (2, 1, 5, 2)):
                b3s[k, slot] = (
                    acc[k, zz(o)] + b1r[k, one].astype(F32) + b2r[k, two].astype(F32)
                ).astype(BF16)
                send(b3s.at[k, slot], b3r.at[k, slot], sem(k, "b3", slot), zz_row(o), x)

        def to_peer(unit):
            send_ = copy(sc.at[c, k, unit], sc.at[c, k, unit], sem(k, "p"), peer, x)
            send_.start()

        def c_send(unit, label, o):
            send(sc.at[c, k, unit], sc.at[c, k, unit], sem(k, *label), zz_row(o), x)

        def c_wait(unit, label):
            arrived(sc.at[c, k, unit], sem(k, *label))

        def final():
            for slot in range(4):
                arrived(b3r.at[k, slot], sem(k, "b3", slot))
            loads[k].wait()
            total = acc[k, z]
            for slot in range(4):
                total = total + b3r[k, slot].astype(F32)
            sc[c, k, z] = (total / (ev[k].astype(F32) + DAMPING)).astype(BF16)
            c_send(z, ("cd", 5), 5)
            c_send(z, ("ce", 5), -5)
            c_send(z, ("cd", 1), 1)
            c_send(z, ("ce", 1), -1)
            to_peer(z)

        def c1():
            for way, t in (("cd", 1), ("ce", -1)):
                for n in (1, 5):
                    c_wait(zz(-t * n), (way, n))
                    c_send(zz(-t * n), (way, n + 2), 2 * t)
            for way, t in (("cd", 1), ("ce", -1)):
                for n in (1, 5):
                    c_send(zz(-t * n), (way, n + 1), t)
                    to_peer(zz(-t * n))

        def c2():
            for way, t in (("cd", 1), ("ce", -1)):
                for n in (3, 7):
                    c_wait(zz(-t * n), (way, n))
                    if (way, n) != ("ce", 7):
                        c_send(zz(-t * n), (way, n + 1), t)
            for t in (1, -1):
                for n in (3, 7):
                    to_peer(zz(-t * n))

        def c3():
            for way, t in (("cd", 1), ("ce", -1)):
                for n in (2, 6, 4, 8):
                    if (way, n) != ("ce", 8):
                        c_wait(zz(-t * n), (way, n))
                        to_peer(zz(-t * n))

        def by_columns(lhs, cols):
            return lax.dot_general(
                lhs, e_v[:, cols], (((1,), (1,)), ((), ())), preferred_element_type=F32)

        def m2():
            p = by_columns(sc[c, k].reshape(NZ * unit_rows, half), own_cols)
            copy(sc.at[other, k], sc.at[other, k], sem(k, "p"), peer, x).wait_recv()
            p = p + by_columns(sc[other, k].reshape(NZ * unit_rows, half), other_cols)
            res[k] = p.reshape(res.shape[1:])
            for slot, o in enumerate((-2, -4, 2)):
                d1s[k, slot] = res[k, xx(o)].astype(BF16)
                to = -1 if o < 0 else 1
                send(d1s.at[k, slot], d1r.at[k, slot], sem(k, "d1", slot), r, xx(to))

        def d2():
            for slot, o, one in ((1, -3, 1), (3, 3, None), (0, -1, 0), (2, 1, 2)):
                value = res[k, xx(o)]
                if one is not None:
                    arrived(d1r.at[k, one], sem(k, "d1", one))
                    value = value + d1r[k, one].astype(F32)
                d2s[k, slot] = value.astype(BF16)
                send(d2s.at[k, slot], d2r.at[k, slot], sem(k, "d2", slot), r, xx(o))

        def df():
            total = res[k, x]
            for slot in range(4):
                arrived(d2r.at[k, slot], sem(k, "d2", slot))
                total = total + d2r[k, slot].astype(F32)
            out[pl.ds(k * h, h)] = total.astype(BF16)

        return [a0, a_round(1), a_round(2), a_round(3), a_round(4), m1, l2, l3, final, c1, c2, c3, m2, d2, df]

    chunks = [steps_of(k) for k in range(CHUNKS)]
    for k in range(CHUNKS):
        chunks[k][0]()
    length = len(chunks[0]) - 1
    for t in range(length + CHUNKS - 1):
        for k in range(CHUNKS):
            if 0 <= t - k < length:
                chunks[k][1 + t - k]()

    for c_ in started:
        c_.wait_send()
    for k in range(CHUNKS):
        copy(sc.at[c, k], sc.at[c, k], sem(k, "p"), CORES * z + other, x).wait_send()


def on_device(grad_slab, eigenbasis, eigenvalues):
    rows, depth = grad_slab.shape
    width = eigenbasis.shape[1]
    half = width // CORES
    h = rows // CHUNKS
    unit_rows = h * NX // NZ
    unit = (unit_rows, half)
    own = (h, depth)
    any_ = pl.BlockSpec(memory_space=pl.ANY)
    vmem = lambda lead, last, kind=BF16: pltpu.VMEM((CHUNKS, *lead, *last), kind)
    return pl.pallas_call(
        kernel,
        out_shape=jax.ShapeDtypeStruct((rows, depth), BF16),
        in_specs=[any_] * 3,
        out_specs=pl.BlockSpec(memory_space=pltpu.VMEM),
        scratch_shapes=[
            pltpu.VMEM(eigenbasis.shape, BF16),
            vmem((NX,), own),
            vmem((), unit),
            vmem((NZ,), unit),
            vmem((NZ,), unit),
            vmem((NZ,), unit, F32),
            vmem((7,), unit),
            vmem((7,), unit),
            vmem((4,), unit),
            vmem((4,), unit),
            vmem((4,), unit),
            vmem((4,), unit),
            pltpu.VMEM((CORES, CHUNKS, NZ, *unit), BF16),
            vmem((NX,), own, F32),
            vmem((3,), own),
            vmem((3,), own),
            vmem((4,), own),
            vmem((4,), own),
            pltpu.SemaphoreType.DMA((1 + 2 * CHUNKS,)),
            pltpu.SemaphoreType.DMA((N_SEMS * CHUNKS,)),
            pltpu.SemaphoreType.DMA((N_SEMS * CHUNKS,)),
        ],
        compiler_params=pltpu.CompilerParams(
            collective_id=0, has_side_effects=True, vmem_limit_bytes=48 * 1024 * 1024
        ),
    )(grad_slab, eigenbasis, eigenvalues)


def solution(mesh):
    return jax.shard_map(
        on_device,
        mesh=mesh,
        in_specs=(P(("ckpt", "col"), "row"), P(("ckpt", "row"), "col"), P("ckpt", "col")),
        out_specs=P(("ckpt", "col"), "row"),
        check_vma=False,
    )
```

time: 315 us -> 125 us (0.40)
  waiting for transfers between devices: 174 us -> 0 us
  Pallas kernels: 0 us -> 120 us
  blocking collectives: 81.1 us -> 0 us
  local copies, waits for them, and re-layouts: 26.9 us -> 4.74 us
  between operations: 13.2 us -> 0.01 us
  matrix products: 8.71 us -> 0 us
  starting transfers between devices: 7.5 us -> 0 us
    reduce_scatter x2 -> x0, waiting for transfers between devices: 138 us -> none  [reduced_to_own(): blocks = lax.psum_scatter(blocks, axes[k], scatter_dimension=0, tiled=True)]
    pallas_call x0 -> x1, Pallas kernels: none -> 120 us  [on_device(): pl.pallas_call(kernel, out_shape=jax.ShapeDtypeStruct((rows, depth), BF16...]
    all_to_all x1 -> x0, blocking collectives: 42.7 us -> none  [summed_on_arrival(): blocks = lax.all_to_all(split_up(value, dim, count), axis, 0, 0, tiled=True)]
    all_gather x1 -> x0, blocking collectives: 38.4 us -> none  [all_blocks(): blocks = lax.all_gather(blocks, axes[k], axis=0, tiled=True)]
    all_gather x1 -> x0, waiting for transfers between devices: 18.8 us -> none  [all_blocks(): blocks = lax.all_gather(blocks, axes[k], axis=0, tiled=True)]
    all_to_all x1 -> x0, waiting for transfers between devices: 16.6 us -> none  [copy_for_each(): return lax.all_to_all(copies, axis, split_axis=0, concat_axis=0, tiled=True)]
    transpose x2 -> x0, local copies, waits for them, and re-layouts: 12.6 us -> none  [the longest x1 7 us: all_blocks(): blocks.transpose(*turned, *range(len(order), blocks.ndim))]
    dot_general x2 -> x0, matrix products: 8.71 us -> none  [the longest x1 4.81 us: on_device(): jnp.dot(gather_directly(grad_slab, 'col', 0), eigenbasis, preferred_eleme...]
  transfers between devices with their start and end apart: 4 -> 0, of which waited for: 4 -> 0; matrix products, arithmetic and copies ran while one was open for 1% -> 0% of each run, Pallas kernels for 0% -> 0%
where the time goes in v1:
time: 125 us
  Pallas kernels  120 us (96%)
  local copies, waits for them, and re-layouts  4.74 us (4%)
    pallas_call x1, Pallas kernels, on_device(): pl.pallas_call(kernel, out_shape=jax.ShapeDtypeStruct((rows, depth), BF16...  120 us
    unnamed x7, local copies, waits for them, and re-layouts  4.74 us

profile of v1, /device:TPU:80, one launch (start us, length us, event | category | flops | bytes accessed | tf_op | source)
XLA Modules:
  0.0 125.2 jit_solution(13441674910365226294)
XLA Ops:
  0.0 0.0 copy-start
  0.0 1.9 %copy-done = bf16[864,1792]{1,0:T(8,128)(2,1)S(1)} copy-done((bf16[864,1792]{1,0:T(8,128)(2,1)S(1)}, bf16[864,1792]{1,0:T(8,128)(2,1)}, u32[]{:S(2)}) %copy-start) | copy-done | bytes 3096600
  1.9 0.0 copy-start.1
  1.9 1.3 %copy-done.1 = bf16[384,1792]{1,0:T(8,128)(2,1)S(1)} copy-done((bf16[384,1792]{1,0:T(8,128)(2,1)S(1)}, bf16[384,1792]{1,0:T(8,128)(2,1)}, u32[]{:S(2)}) %copy-start.1) | copy-done | bytes 1376280
  3.2 0.0 copy-start.2
  3.2 0.9 copy-done.2
  4.1 120.4 %shard_map.37 = bf16[48,864]{1,0:T(8,128)(2,1)S(1)} custom-call(bf16[48,864]{1,0:T(8,128)(2,1)S(1)} %copy-done.2, bf16[864,1792]{1,0:T(8,128)(2,1)S(1)} %copy-done, bf16[384,1792]{1,0:T(8,128)(2,1)S(1)} %copy-done.1), custom_call_target="tpu_custom_call" | custom-call | tf_op jit(solution)/shard_map/pallas_call | solution.py:269
  124.6 0.6 copy.5
Async XLA Ops:
  0.0 1.9 %copy-start = (bf16[864,1792]{1,0:T(8,128)(2,1)S(1)}, bf16[864,1792]{1,0:T(8,128)(2,1)}, u32[]{:S(2)}) copy-start(bf16[864,1792]{1,0:T(8,128)(2,1)} %eig.1) | copy-start | bytes 9289732
  1.9 1.3 %copy-start.1 = (bf16[384,1792]{1,0:T(8,128)(2,1)S(1)}, bf16[384,1792]{1,0:T(8,128)(2,1)}, u32[]{:S(2)}) copy-start(bf16[384,1792]{1,0:T(8,128)(2,1)} %values.1) | copy-start | bytes 4128772
  3.2 0.9 copy-start.2

commit v2 on v1

--- a/solution.py
+++ b/solution.py
@@ -16,6 +16,11 @@
 BF16 = jnp.bfloat16
 F32 = jnp.float32
 N_SEMS = 48
+GAP = 3.3
+LEVEL_ONE = (
+    ("fa", 1, (-5, 7)), ("fb", -1, (-7, 5)), ("fc", -2, (-8,)),
+    ("na", 1, (-1, 3)), ("nb", -1, (-3, 1)), ("nc", -2, (-4,)), ("nd", 2, (4,)),
+)
 
 
 class Labels:
@@ -29,7 +34,7 @@
 def kernel(
     grad, eig, values, out,
     e_v, g_all, ev, psend, precv, acc,
-    b1s, b1r, b2s, b2r, b3s, b3r, sc, res, d1s, d1r, d2s, d2r,
+    b1s, b1r, b2s, b2r, sc, res, d1s, d1r, d2s, d2r,
     local_sem, send_sem, recv_sem,
 ):
     r = lax.axis_index("row")
@@ -83,7 +88,7 @@
 
     barrier = pltpu.get_barrier_semaphore()
     partners = [(CORES * z + other, x)]
-    partners += [(zrow(o), x) for o in (1, -1, 2, -2, 5, -5)]
+    partners += [(zrow(o), x) for o in (1, -1, 2, -2, 6, -6)]
     partners += [(r, xcol(o)) for o in (1, -1, 3, -3)]
     for row, col in partners:
         pl.semaphore_signal(barrier, inc=1, device_id={"row": row, "col": col}, device_id_type=MESH)
@@ -106,20 +111,24 @@
 
         def a0():
             own_g[k].wait()
-            a_send(x, ("ad", 1), xx(1))
-            a_send(x, ("ae", 1), xx(-1))
-
-        def a_round(n):
-            def step():
-                a_wait(xx(-n), ("ad", n))
-                if n < 4:
-                    a_send(xx(-n), ("ad", n + 1), xx(1))
-                    a_wait(xx(n), ("ae", n))
-                    if n < 3:
-                        a_send(xx(n), ("ae", n + 1), xx(-1))
-            return step
+            for way, t in (("ad", 1), ("ae", -1)):
+                for n in (3, 1):
+                    a_send(x, (way, n), xx(t * n))
+
+        def a_near():
+            for way, t in (("ad", 1), ("ae", -1)):
+                a_wait(xx(-t), (way, 1))
+                a_send(xx(-t), (way, 2), xx(t))
+
+        def a_far():
+            a_wait(xx(-3), ("ad", 3))
+            a_send(xx(-3), ("ad", 4), xx(1))
+            a_wait(xx(3), ("ae", 3))
 
         def m1():
+            a_wait(xx(-2), ("ad", 2))
+            a_wait(xx(2), ("ae", 2))
+            a_wait(xx(-4), ("ad", 4))
             if k == 0:
                 load_e.wait()
             g = g_all[k].reshape(NX * h, g_all.shape[3])
@@ -128,35 +137,37 @@
             send(psend.at[k], precv.at[k], sem(k, "x"), peer, x)
             p = jnp.dot(g, e_v[:, own_cols], preferred_element_type=F32)
             acc[k] = p.reshape(acc.shape[1:])
+
+        def m1_sum():
             arrived(precv.at[k], sem(k, "x"))
             acc[k] = acc[k] + precv[k].astype(F32)
-            for slot, d in enumerate((4, 8, 2, 6)):
-                b1s[k, slot] = acc[k, zz(-d)].astype(BF16)
-            for slot, e in enumerate((4, 2, 6)):
-                b1s[k, 4 + slot] = acc[k, zz(e)].astype(BF16)
-            for name, lo, n, to in (("b1a", 0, 2, -1), ("b1b", 4, 1, 1), ("b1c", 2, 2, -1), ("b1d", 5, 2, 1)):
-                send(b1s.at[k, pl.ds(lo, n)], b1r.at[k, pl.ds(lo, n)], sem(k, name), zz_row(to), x)
-
-        def l2():
-            arrived(b1r.at[k, pl.ds(0, 2)], sem(k, "b1a"))
-            arrived(b1r.at[k, pl.ds(4, 1)], sem(k, "b1b"))
-            for slot, d in enumerate((3, 7)):
-                b2s[k, slot] = (acc[k, zz(-d)] + b1r[k, slot].astype(F32)).astype(BF16)
-            b2s[k, 2] = (acc[k, zz(3)] + b1r[k, 4].astype(F32)).astype(BF16)
-            b2s[k, 3] = acc[k, zz(7)].astype(BF16)
-            for name, lo, to in (("b2a", 0, -2), ("b2b", 2, 2)):
-                send(b2s.at[k, pl.ds(lo, 2)], b2r.at[k, pl.ds(lo, 2)], sem(k, name), zz_row(to), x)
-
-        def l3():
-            arrived(b1r.at[k, pl.ds(2, 2)], sem(k, "b1c"))
-            arrived(b1r.at[k, pl.ds(5, 2)], sem(k, "b1d"))
-            arrived(b2r.at[k, pl.ds(0, 2)], sem(k, "b2a"))
-            arrived(b2r.at[k, pl.ds(2, 2)], sem(k, "b2b"))
-            for slot, o, one, two in ((1, -5, 3, 1), (3, 5, 6, 3), (0, -1, 2, 0), (2, 1, 5, 2)):
-                b3s[k, slot] = (
-                    acc[k, zz(o)] + b1r[k, one].astype(F32) + b2r[k, two].astype(F32)
-                ).astype(BF16)
-                send(b3s.at[k, slot], b3r.at[k, slot], sem(k, "b3", slot), zz_row(o), x)
+            slot = 0
+            for name, to, units in LEVEL_ONE:
+                for o in units:
+                    b1s[k, slot] = acc[k, zz(o)].astype(BF16)
+                    slot += 1
+                n = len(units)
+                part = pl.ds(slot - n, n)
+                send(b1s.at[k, part], b1r.at[k, part], sem(k, name), zz_row(to), x)
+
+        def meet(names, sums):
+            slot = 0
+            for name, to, units in LEVEL_ONE:
+                if name in names:
+                    arrived(b1r.at[k, pl.ds(slot, len(units))], sem(k, name))
+                slot += len(units)
+            for slot, o, ones in sums:
+                value = acc[k, zz(o)]
+                for one in ones:
+                    value = value + b1r[k, one].astype(F32)
+                b2s[k, slot] = value.astype(BF16)
+                send(b2s.at[k, slot], b2r.at[k, slot], sem(k, "b2", slot), zz_row(o), x)
+
+        def meet_far():
+            meet(("fa", "fb", "fc"), ((1, -6, (0, 2, 4)), (3, 6, (3, 1))))
+
+        def meet_near():
+            meet(("na", "nb", "nc", "nd"), ((0, -2, (5, 7, 9)), (2, 2, (8, 6, 10))))
 
         def to_peer(unit):
             send_ = copy(sc.at[c, k, unit], sc.at[c, k, unit], sem(k, "p"), peer, x)
@@ -170,41 +181,36 @@
 
         def final():
             for slot in range(4):
-                arrived(b3r.at[k, slot], sem(k, "b3", slot))
+                arrived(b2r.at[k, slot], sem(k, "b2", slot))
             loads[k].wait()
             total = acc[k, z]
             for slot in range(4):
-                total = total + b3r[k, slot].astype(F32)
+                total = total + b2r[k, slot].astype(F32)
             sc[c, k, z] = (total / (ev[k].astype(F32) + DAMPING)).astype(BF16)
-            c_send(z, ("cd", 5), 5)
-            c_send(z, ("ce", 5), -5)
-            c_send(z, ("cd", 1), 1)
-            c_send(z, ("ce", 1), -1)
+            for n in (6, 2):
+                for way, t in (("cd", 1), ("ce", -1)):
+                    c_send(z, (way, n), t * n)
             to_peer(z)
 
-        def c1():
+        def fan(n):
             for way, t in (("cd", 1), ("ce", -1)):
-                for n in (1, 5):
-                    c_wait(zz(-t * n), (way, n))
-                    c_send(zz(-t * n), (way, n + 2), 2 * t)
-            for way, t in (("cd", 1), ("ce", -1)):
-                for n in (1, 5):
-                    c_send(zz(-t * n), (way, n + 1), t)
-                    to_peer(zz(-t * n))
-
-        def c2():
-            for way, t in (("cd", 1), ("ce", -1)):
-                for n in (3, 7):
-                    c_wait(zz(-t * n), (way, n))
-                    if (way, n) != ("ce", 7):
-                        c_send(zz(-t * n), (way, n + 1), t)
+                unit = zz(-t * n)
+                c_wait(unit, (way, n))
+                for m in (2, -1, 1):
+                    if (way, n + m) != ("ce", 8):
+                        c_send(unit, (way, n + m), t * m)
             for t in (1, -1):
-                for n in (3, 7):
-                    to_peer(zz(-t * n))
-
-        def c3():
-            for way, t in (("cd", 1), ("ce", -1)):
-                for n in (2, 6, 4, 8):
+                to_peer(zz(-t * n))
+
+        def c_near():
+            fan(2)
+
+        def c_far():
+            fan(6)
+
+        def c_end():
+            for n in (1, 3, 4, 5, 7, 8):
+                for way, t in (("cd", 1), ("ce", -1)):
                     if (way, n) != ("ce", 8):
                         c_wait(zz(-t * n), (way, n))
                         to_peer(zz(-t * n))
@@ -239,16 +245,17 @@
                 total = total + d2r[k, slot].astype(F32)
             out[pl.ds(k * h, h)] = total.astype(BF16)
 
-        return [a0, a_round(1), a_round(2), a_round(3), a_round(4), m1, l2, l3, final, c1, c2, c3, m2, d2, df]
-
-    chunks = [steps_of(k) for k in range(CHUNKS)]
+        return [
+            (0.0, a0), (3.4, a_near), (6.0, a_far), (9.5, m1), (11.5, m1_sum),
+            (16.5, meet_far), (17.0, meet_near), (25.0, final),
+            (29.5, c_near), (33.0, c_far), (37.0, c_end), (37.1, m2), (42.0, d2), (48.0, df),
+        ]
+
+    plan = []
     for k in range(CHUNKS):
-        chunks[k][0]()
-    length = len(chunks[0]) - 1
-    for t in range(length + CHUNKS - 1):
-        for k in range(CHUNKS):
-            if 0 <= t - k < length:
-                chunks[k][1 + t - k]()
+        plan += [(at + GAP * k, k, step) for at, step in steps_of(k)]
+    for _, _, step in sorted(plan, key=lambda item: item[:2]):
+        step()
 
     for c_ in started:
         c_.wait_send()
@@ -264,7 +271,7 @@
     unit_rows = h * NX // NZ
     unit = (unit_rows, half)
     own = (h, depth)
-    any_ = pl.BlockSpec(memory_space=pl.ANY)
+    any_ = pl.BlockSpec(memory_space=pltpu.HBM)
     vmem = lambda lead, last, kind=BF16: pltpu.VMEM((CHUNKS, *lead, *last), kind)
     return pl.pallas_call(
         kernel,
@@ -278,10 +285,8 @@
             vmem((NZ,), unit),
             vmem((NZ,), unit),
             vmem((NZ,), unit, F32),
-            vmem((7,), unit),
-            vmem((7,), unit),
-            vmem((4,), unit),
-            vmem((4,), unit),
+            vmem((11,), unit),
+            vmem((11,), unit),
             vmem((4,), unit),
             vmem((4,), unit),
             pltpu.VMEM((CORES, CHUNKS, NZ, *unit), BF16),
@@ -295,7 +300,7 @@
             pltpu.SemaphoreType.DMA((N_SEMS * CHUNKS,)),
         ],
         compiler_params=pltpu.CompilerParams(
-            collective_id=0, has_side_effects=True, vmem_limit_bytes=48 * 1024 * 1024
+            collective_id=0, has_side_effects=True, vmem_limit_bytes=67043328
         ),
     )(grad_slab, eigenbasis, eigenvalues)
 

time: 125 us -> 109 us (0.87)
  Pallas kernels: 120 us -> 107 us
  local copies, waits for them, and re-layouts: 4.74 us -> 1.53 us
    pallas_call x1, Pallas kernels: 120 us -> 107 us  [on_device(): pl.pallas_call(kernel, out_shape=jax.ShapeDtypeStruct((rows, depth), BF16...]
    unnamed x7 -> x1, local copies, waits for them, and re-layouts: 4.74 us -> 1.53 us
where the time goes in v2:
time: 109 us
  Pallas kernels  107 us (98%)
  local copies, waits for them, and re-layouts  1.53 us (1%)
    pallas_call x1, Pallas kernels, on_device(): pl.pallas_call(kernel, out_shape=jax.ShapeDtypeStruct((rows, depth), BF16...  107 us

profile of v2, /device:TPU:80, one launch (start us, length us, event | category | flops | bytes accessed | tf_op | source)
XLA Modules:
  0.0 108.6 jit_solution(4153014766185686546)
XLA Ops:
  0.0 107.0 %shard_map.37 = bf16[48,864]{1,0:T(8,128)(2,1)} custom-call(bf16[48,864]{1,0:T(8,128)(2,1)} %grad.1, bf16[864,1792]{1,0:T(8,128)(2,1)} %eig.1, bf16[384,1792]{1,0:T(8,128)(2,1)} %values.1), custom_call_target="tpu_custom_call" | custom-call | tf_op jit(solution)/shard_map/pallas_call | solution.py:276
  107.0 1.5 %copy.5 = bf16[48,864]{1,0:T(8,128)(2,1)} copy(bf16[48,864]{1,0:T(8,128)(2,1)} %shard_map.37) | data formatting | bytes 165888

commit v3 on v2

v3 whole, which is shorter than its diff:
```python
import functools

import jax
import jax.numpy as jnp
from jax import lax
from jax.experimental import pallas as pl
from jax.experimental.pallas import tpu as pltpu
from jax.sharding import PartitionSpec as P

DAMPING = 0.1
MESH = pl.DeviceIdType.MESH
CORES = 2
CHUNKS = 3
NZ = 16
NX = 8
BF16 = jnp.bfloat16
F32 = jnp.float32
SENT = ("g", "x", "b1", "b2", "b3", "c", "p", "d1", "d2")
ARRIVE = ("a2", "a", "x", "far", "near", "b2", "b3", "c3", "c6", "c", "p", "d1", "d2")
GAP = 3.7
LEVEL_ONE = (
    ("far", 1, (-5, 7)), ("far", -1, (-7, 5)), ("far", -2, (-8,)),
    ("near", 1, (-2, 4)), ("near", -1, (-4, 2)),
)


def kernel(
    grad, eig, values, out,
    e_v, g_all, ev, psend, precv, acc,
    b1s, b1r, b2s, b2r, b3s, b3r, sc, res, d1s, d1r, d2s, d2r,
    local_sem, send_sem, recv_sem,
):
    r = lax.axis_index("row")
    x = lax.axis_index("col")
    z, c = lax.div(r, CORES), lax.rem(r, CORES)
    other = 1 - c
    unit_rows, half = acc.shape[2], acc.shape[3]
    h = g_all.shape[2]

    def send(k, src, dst, sent, arrive, row, col):
        pltpu.make_async_remote_copy(
            src_ref=src, dst_ref=dst, send_sem=send_sem.at[SENT.index(sent)],
            recv_sem=recv_sem.at[k * len(ARRIVE) + ARRIVE.index(arrive)],
            device_id={"row": row, "col": col}, device_id_type=MESH,
        ).start()

    def pending(ref, sent=0, arrive=0):
        return pltpu.make_async_remote_copy(
            src_ref=ref, dst_ref=ref, send_sem=send_sem.at[sent], recv_sem=recv_sem.at[arrive],
            device_id={"row": CORES * z + other, "col": x}, device_id_type=MESH,
        )

    def arrived(k, ref, arrive):
        pending(ref, arrive=k * len(ARRIVE) + ARRIVE.index(arrive)).wait_recv()

    def all_sent(ref, sent):
        pending(ref, sent=SENT.index(sent)).wait_send()

    def zrow(offset):
        return lax.rem(z + (offset + NZ), NZ) * CORES + c

    def zunit(offset):
        return lax.rem(z + (offset + NZ), NZ)

    def xcol(offset):
        return lax.rem(x + (offset + NX), NX)

    for k in range(CHUNKS):
        pltpu.make_async_copy(grad.at[pl.ds(k * h, h)], g_all.at[k, x], local_sem.at[0]).start()
    pltpu.make_async_copy(eig, e_v, local_sem.at[1]).start()
    block = lax.div(z, 2)
    for k in range(CHUNKS):
        first = block * (CHUNKS * h) + k * h + lax.rem(z, 2) * unit_rows
        pltpu.make_async_copy(
            values.at[pl.ds(pl.multiple_of(first, unit_rows), unit_rows),
                      pl.ds(pl.multiple_of(c * half, 128), half)],
            ev.at[k], local_sem.at[2]).start()

    def loaded(ref, index):
        pltpu.make_async_copy(ref, ref, local_sem.at[index]).wait()

    barrier = pltpu.get_barrier_semaphore()
    partners = [(CORES * z + other, x)]
    partners += [(zrow(o), x) for o in (1, -1, 2, -2, 3, -3)]
    partners += [(r, xcol(o)) for o in (1, -1, 2, -2)]
    for row, col in partners:
        pl.semaphore_signal(barrier, inc=1, device_id={"row": row, "col": col}, device_id_type=MESH)
    pl.semaphore_wait(barrier, len(partners))

    def steps_of(k):
        s = -1 if k % 2 else 1
        zz_row = lambda o: zrow(s * o)
        zz = lambda o: zunit(s * o)
        xx = lambda o: xcol(s * o)
        own_cols = pl.ds(pl.multiple_of(c * half, 128), half)
        other_cols = pl.ds(pl.multiple_of(other * half, 128), half)
        peer = CORES * z + other

        def a_send(o, n, to):
            block_at = g_all.at[k, xx(o)]
            send(k, block_at, block_at, "g", "a2" if n == 2 else "a", r, xx(to))

        def a0():
            if k == 0:
                loaded(g_all.at[:, x], 0)
            for n in (2, 1):
                a_send(0, n, n)
                a_send(0, n, -n)

        def a_pass():
            arrived(k, g_all.at[k, pl.ds(0, 2)], "a2")
            a_send(-2, 4, 2)
            a_send(-2, 3, 1)
            a_send(2, 3, -1)

        def m1():
            arrived(k, g_all.at[k, pl.ds(0, 5)], "a")
            if k == 0:
                loaded(e_v, 1)
            g = g_all[k].reshape(NX * h, g_all.shape[3])
            p = jnp.dot(g, e_v[:, other_cols], preferred_element_type=F32)
            psend[k] = p.astype(BF16).reshape(psend.shape[1:])
            send(k, psend.at[k], precv.at[k], "x", "x", peer, x)
            p = jnp.dot(g, e_v[:, own_cols], preferred_element_type=F32)
            acc[k] = p.reshape(acc.shape[1:])

        def m1_sum():
            arrived(k, precv.at[k], "x")
            acc[k] = acc[k] + precv[k].astype(F32)
            slot = 0
            for arrive, to, units in LEVEL_ONE:
                for o in units:
                    b1s[k, slot] = acc[k, zz(o)].astype(BF16)
                    slot += 1
                n = len(units)
                part = pl.ds(slot - n, n)
                send(k, b1s.at[k, part], b1r.at[k, part], "b1", arrive, zz_row(to), x)
            for slot, o in ((2, -1), (3, 1)):
                b3s[k, slot] = acc[k, zz(o)].astype(BF16)
                send(k, b3s.at[k, slot], b3r.at[k, slot], "b3", "b3", zz_row(o), x)

        def level_one_sum(o, slots):
            value = acc[k, zz(o)]
            for slot in slots:
                value = value + b1r[k, slot].astype(F32)
            return value

        def meet_far():
            arrived(k, b1r.at[k, pl.ds(0, 5)], "far")
            for slot, o, slots, to in ((0, -6, (0, 2, 4), -3), (1, 6, (3, 1), 3)):
                b2s[k, slot] = level_one_sum(o, slots).astype(BF16)
                send(k, b2s.at[k, slot], b2r.at[k, slot], "b2", "b2", zz_row(to), x)

        def meet_near():
            arrived(k, b1r.at[k, pl.ds(5, 4)], "near")
            arrived(k, b2r.at[k], "b2")
            for slot, o, slots in ((0, -3, (5, 7)), (1, 3, (8, 6))):
                value = level_one_sum(o, slots) + b2r[k, slot].astype(F32)
                b3s[k, slot] = value.astype(BF16)
                send(k, b3s.at[k, slot], b3r.at[k, slot], "b3", "b3", zz_row(o), x)

        def to_peer(unit):
            at = sc.at[c, k, unit]
            send(k, at, at, "p", "p", peer, x)

        def c_send(unit, n, o):
            at = sc.at[c, k, unit]
            send(k, at, at, "c", "c%d" % n if n in (3, 6) else "c", zz_row(o), x)

        def final():
            arrived(k, b3r.at[k], "b3")
            if k == 0:
                loaded(ev, 2)
            total = acc[k, z]
            for slot in range(4):
                total = total + b3r[k, slot].astype(F32)
            sc[c, k, z] = (total / (ev[k].astype(F32) + DAMPING)).astype(BF16)
            for n in (3, 1):
                c_send(z, n, n)
                c_send(z, n, -n)
            to_peer(z)

        def fan(n, moves):
            arrived(k, sc.at[c, k, pl.ds(0, 2)], "c%d" % n)
            for t in (1, -1):
                for m in moves:
                    if t * (n + m) != -8:
                        c_send(zz(-t * n), n + m, t * m)
            for t in (1, -1):
                to_peer(zz(-t * n))

        def c_near():
            fan(3, (3, -1, 1))

        def c_far():
            fan(6, (2, -1, 1))

        def c_end():
            arrived(k, sc.at[c, k, pl.ds(0, 11)], "c")
            for n in (1, 2, 4, 5, 7, 8):
                for t in (1, -1):
                    if t * n != -8:
                        to_peer(zz(-t * n))

        def by_columns(lhs, cols):
            return lax.dot_general(
                lhs, e_v[:, cols], (((1,), (1,)), ((), ())), preferred_element_type=F32)

        def m2():
            p = by_columns(sc[c, k].reshape(NZ * unit_rows, half), own_cols)
            arrived(k, sc.at[other, k], "p")
            p = p + by_columns(sc[other, k].reshape(NZ * unit_rows, half), other_cols)
            res[k] = p.reshape(res.shape[1:])
            for slot, o, to in ((0, -4, -2), (1, -3, -1), (2, 3, 1)):
                d1s[k, slot] = res[k, xx(o)].astype(BF16)
                send(k, d1s.at[k, slot], d1r.at[k, slot], "d1", "d1", r, xx(to))
            for slot, o in ((2, -1), (3, 1)):
                d2s[k, slot] = res[k, xx(o)].astype(BF16)
                send(k, d2s.at[k, slot], d2r.at[k, slot], "d2", "d2", r, xx(o))

        def d2():
            arrived(k, d1r.at[k], "d1")
            for slot, o, ones in ((0, -2, (0, 1)), (1, 2, (2,))):
                value = res[k, xx(o)]
                for one in ones:
                    value = value + d1r[k, one].astype(F32)
                d2s[k, slot] = value.astype(BF16)
                send(k, d2s.at[k, slot], d2r.at[k, slot], "d2", "d2", r, xx(o))

        def df():
            arrived(k, d2r.at[k], "d2")
            total = res[k, x]
            for slot in range(4):
                total = total + d2r[k, slot].astype(F32)
            out[pl.ds(k * h, h)] = total.astype(BF16)

        return [
            (0.0, a0), (5.0, a_pass), (9.0, m1), (11.5, m1_sum),
            (16.0, meet_far), (21.0, meet_near), (26.0, final),
            (31.0, c_near), (36.0, c_far), (40.5, c_end), (40.6, m2), (46.0, d2), (51.0, df),
        ]

    plan = []
    for k in range(CHUNKS):
        plan += [(at + GAP * k, k, step) for at, step in steps_of(k)]
    for _, _, step in sorted(plan, key=lambda item: item[:2]):
        step()

    for ref, sent in (
        (g_all.at[:, pl.ds(0, NX - 1)], "g"), (psend, "x"), (b1s, "b1"), (b2s, "b2"), (b3s, "b3"),
        (sc.at[c, :, pl.ds(0, NZ - 1)], "c"), (sc.at[c], "p"), (d1s, "d1"), (d2s, "d2"),
    ):
        all_sent(ref, sent)


def on_device(grad_slab, eigenbasis, eigenvalues):
    rows, depth = grad_slab.shape
    width = eigenbasis.shape[1]
    half = width // CORES
    h = rows // CHUNKS
    unit_rows = h * NX // NZ
    unit = (unit_rows, half)
    own = (h, depth)
    any_ = pl.BlockSpec(memory_space=pltpu.HBM)
    vmem = lambda lead, last, kind=BF16: pltpu.VMEM((CHUNKS, *lead, *last), kind)
    return pl.pallas_call(
        kernel,
        out_shape=jax.ShapeDtypeStruct((rows, depth), BF16),
        in_specs=[any_] * 3,
        out_specs=pl.BlockSpec(memory_space=pltpu.VMEM),
        scratch_shapes=[
            pltpu.VMEM(eigenbasis.shape, BF16),
            vmem((NX,), own),
            vmem((), unit),
            vmem((NZ,), unit),
            vmem((NZ,), unit),
            vmem((NZ,), unit, F32),
            vmem((9,), unit),
            vmem((9,), unit),
            vmem((2,), unit),
            vmem((2,), unit),
            vmem((4,), unit),
            vmem((4,), unit),
            pltpu.VMEM((CORES, CHUNKS, NZ, *unit), BF16),
            vmem((NX,), own, F32),
            vmem((3,), own),
            vmem((3,), own),
            vmem((4,), own),
            vmem((4,), own),
            pltpu.SemaphoreType.DMA((3,)),
            pltpu.SemaphoreType.DMA((len(SENT),)),
            pltpu.SemaphoreType.DMA((CHUNKS * len(ARRIVE),)),
        ],
        compiler_params=pltpu.CompilerParams(
            collective_id=0, has_side_effects=True, vmem_limit_bytes=67043328
        ),
    )(grad_slab, eigenbasis, eigenvalues)


def solution(mesh):
    return jax.shard_map(
        on_device,
        mesh=mesh,
        in_specs=(P(("ckpt", "col"), "row"), P(("ckpt", "row"), "col"), P("ckpt", "col")),
        out_specs=P(("ckpt", "col"), "row"),
        check_vma=False,
    )
```

time: 109 us -> 104 us (0.954)
  Pallas kernels: 107 us -> 102 us
    pallas_call x1, Pallas kernels: 107 us -> 102 us  [on_device(): pl.pallas_call(kernel, out_shape=jax.ShapeDtypeStruct((rows, depth), BF16...]
where the time goes in v3:
time: 104 us
  Pallas kernels  102 us (98%)
  local copies, waits for them, and re-layouts  1.53 us (1%)
    pallas_call x1, Pallas kernels, on_device(): pl.pallas_call(kernel, out_shape=jax.ShapeDtypeStruct((rows, depth), BF16...  102 us

profile of v3, /device:TPU:80, one launch (start us, length us, event | category | flops | bytes accessed | tf_op | source)
XLA Modules:
  0.0 103.8 jit_solution(8606149611920391482)
XLA Ops:
  0.0 102.2 %shard_map.37 = bf16[48,864]{1,0:T(8,128)(2,1)} custom-call(bf16[48,864]{1,0:T(8,128)(2,1)} %grad.1, bf16[864,1792]{1,0:T(8,128)(2,1)} %eig.1, bf16[384,1792]{1,0:T(8,128)(2,1)} %values.1), custom_call_target="tpu_custom_call" | custom-call | tf_op jit(solution)/shard_map/pallas_call | solution.py:266
  102.3 1.5 %copy.5 = bf16[48,864]{1,0:T(8,128)(2,1)} copy(bf16[48,864]{1,0:T(8,128)(2,1)} %shard_map.37) | data formatting | bytes 165888

commit v4 on v3

--- a/solution.py
+++ b/solution.py
@@ -15,20 +15,30 @@
 NX = 8
 BF16 = jnp.bfloat16
 F32 = jnp.float32
-SENT = ("g", "x", "b1", "b2", "b3", "c", "p", "d1", "d2")
-ARRIVE = ("a2", "a", "x", "far", "near", "b2", "b3", "c3", "c6", "c", "p", "d1", "d2")
-GAP = 3.7
+SENT = ("g", "x", "b1", "b3", "c", "p", "d1", "d2")
+ARRIVE = ("a2", "a", "x", "far", "near", "b3", "c2", "c5", "c", "p", "d1", "d2")
 LEVEL_ONE = (
-    ("far", 1, (-5, 7)), ("far", -1, (-7, 5)), ("far", -2, (-8,)),
-    ("near", 1, (-2, 4)), ("near", -1, (-4, 2)),
+    ("far", -3, (-8,)), ("far", 1, (-4, 6)), ("far", -1, (-6, 4)), ("far", -2, (-7,)), ("far", 2, (7,)),
+    ("near", 1, (-1, 3)), ("near", -1, (-3, 1)),
+)
+ORDER = (
+    (0, "a0"), (1, "a0"), (None, "hello_1"), (0, "a_pass"), (None, "hello_2"),
+    (2, "a0"), (1, "a_pass"), (0, "m1"), (0, "m1_sum"), (2, "a_pass"),
+    (1, "m1"), (1, "m1_sum"), (2, "m1"), (None, "hello_3"), (0, "meet_far"),
+    (2, "m1_sum"), (1, "meet_far"), (0, "meet_near"), (1, "meet_near"), (2, "meet_far"),
+    (2, "meet_near"), (0, "final"), (1, "final"), (2, "final"), (0, "c_near"),
+    (0, "c_far"), (1, "c_near"), (1, "c_far"), (2, "c_near"), (2, "c_far"),
+    (0, "c_end"), (0, "m2"), (1, "c_end"), (2, "c_end"), (1, "m2"),
+    (2, "m2"), (0, "d2"), (1, "d2"), (2, "d2"), (0, "df"),
+    (1, "df"), (2, "df"),
 )
 
 
 def kernel(
     grad, eig, values, out,
     e_v, g_all, ev, psend, precv, acc,
-    b1s, b1r, b2s, b2r, b3s, b3r, sc, res, d1s, d1r, d2s, d2r,
-    local_sem, send_sem, recv_sem,
+    b1s, b1r, b3s, b3r, sc, res, d1s, d1r, d2s, d2r,
+    local_sem, send_sem, recv_sem, word_sem,
 ):
     r = lax.axis_index("row")
     x = lax.axis_index("col")
@@ -81,11 +91,29 @@
 
     barrier = pltpu.get_barrier_semaphore()
     partners = [(CORES * z + other, x)]
-    partners += [(zrow(o), x) for o in (1, -1, 2, -2, 3, -3)]
+    partners += [(zrow(o), x) for o in (1, -1)]
     partners += [(r, xcol(o)) for o in (1, -1, 2, -2)]
     for row, col in partners:
         pl.semaphore_signal(barrier, inc=1, device_id={"row": row, "col": col}, device_id_type=MESH)
     pl.semaphore_wait(barrier, len(partners))
+
+    def pass_word(i, hops):
+        for o in (hops, -hops):
+            pl.semaphore_signal(
+                word_sem.at[i], inc=1, device_id={"row": zrow(o), "col": x}, device_id_type=MESH)
+
+    def hello_1():
+        pl.semaphore_wait(word_sem.at[0], 2)
+        pass_word(1, 1)
+
+    def hello_2():
+        pl.semaphore_wait(word_sem.at[1], 2)
+        pass_word(2, 2)
+
+    def hello_3():
+        pl.semaphore_wait(word_sem.at[2], 2)
+
+    pass_word(0, 1)
 
     def steps_of(k):
         s = -1 if k % 2 else 1
@@ -135,9 +163,6 @@
                 n = len(units)
                 part = pl.ds(slot - n, n)
                 send(k, b1s.at[k, part], b1r.at[k, part], "b1", arrive, zz_row(to), x)
-            for slot, o in ((2, -1), (3, 1)):
-                b3s[k, slot] = acc[k, zz(o)].astype(BF16)
-                send(k, b3s.at[k, slot], b3r.at[k, slot], "b3", "b3", zz_row(o), x)
 
         def level_one_sum(o, slots):
             value = acc[k, zz(o)]
@@ -145,19 +170,17 @@
                 value = value + b1r[k, slot].astype(F32)
             return value
 
+        def meet(lo, n, arrive, sums):
+            arrived(k, b1r.at[k, pl.ds(lo, n)], arrive)
+            for slot, o, slots in sums:
+                b3s[k, slot] = level_one_sum(o, slots).astype(BF16)
+                send(k, b3s.at[k, slot], b3r.at[k, slot], "b3", "b3", zz_row(o), x)
+
         def meet_far():
-            arrived(k, b1r.at[k, pl.ds(0, 5)], "far")
-            for slot, o, slots, to in ((0, -6, (0, 2, 4), -3), (1, 6, (3, 1), 3)):
-                b2s[k, slot] = level_one_sum(o, slots).astype(BF16)
-                send(k, b2s.at[k, slot], b2r.at[k, slot], "b2", "b2", zz_row(to), x)
+            meet(0, 7, "far", ((0, -5, (0, 1, 3, 5)), (1, 5, (2, 4, 6))))
 
         def meet_near():
-            arrived(k, b1r.at[k, pl.ds(5, 4)], "near")
-            arrived(k, b2r.at[k], "b2")
-            for slot, o, slots in ((0, -3, (5, 7)), (1, 3, (8, 6))):
-                value = level_one_sum(o, slots) + b2r[k, slot].astype(F32)
-                b3s[k, slot] = value.astype(BF16)
-                send(k, b3s.at[k, slot], b3r.at[k, slot], "b3", "b3", zz_row(o), x)
+            meet(7, 4, "near", ((2, -2, (7, 9)), (3, 2, (8, 10))))
 
         def to_peer(unit):
             at = sc.at[c, k, unit]
@@ -165,7 +188,7 @@
 
         def c_send(unit, n, o):
             at = sc.at[c, k, unit]
-            send(k, at, at, "c", "c%d" % n if n in (3, 6) else "c", zz_row(o), x)
+            send(k, at, at, "c", "c%d" % n if n in (2, 5) else "c", zz_row(o), x)
 
         def final():
             arrived(k, b3r.at[k], "b3")
@@ -175,7 +198,7 @@
             for slot in range(4):
                 total = total + b3r[k, slot].astype(F32)
             sc[c, k, z] = (total / (ev[k].astype(F32) + DAMPING)).astype(BF16)
-            for n in (3, 1):
+            for n in (5, 2):
                 c_send(z, n, n)
                 c_send(z, n, -n)
             to_peer(z)
@@ -190,14 +213,14 @@
                 to_peer(zz(-t * n))
 
         def c_near():
-            fan(3, (3, -1, 1))
+            fan(2, (-1, 1))
 
         def c_far():
-            fan(6, (2, -1, 1))
+            fan(5, (3, 2, -1, 1))
 
         def c_end():
             arrived(k, sc.at[c, k, pl.ds(0, 11)], "c")
-            for n in (1, 2, 4, 5, 7, 8):
+            for n in (1, 3, 4, 6, 7, 8):
                 for t in (1, -1):
                     if t * n != -8:
                         to_peer(zz(-t * n))
@@ -234,20 +257,16 @@
                 total = total + d2r[k, slot].astype(F32)
             out[pl.ds(k * h, h)] = total.astype(BF16)
 
-        return [
-            (0.0, a0), (5.0, a_pass), (9.0, m1), (11.5, m1_sum),
-            (16.0, meet_far), (21.0, meet_near), (26.0, final),
-            (31.0, c_near), (36.0, c_far), (40.5, c_end), (40.6, m2), (46.0, d2), (51.0, df),
-        ]
-
-    plan = []
-    for k in range(CHUNKS):
-        plan += [(at + GAP * k, k, step) for at, step in steps_of(k)]
-    for _, _, step in sorted(plan, key=lambda item: item[:2]):
-        step()
+        steps = (a0, a_pass, m1, m1_sum, meet_far, meet_near, final, c_near, c_far, c_end, m2, d2, df)
+        return {step.__name__: step for step in steps}
+
+    chunks = {k: steps_of(k) for k in range(CHUNKS)}
+    chunks[None] = {step.__name__: step for step in (hello_1, hello_2, hello_3)}
+    for k, name in ORDER:
+        chunks[k][name]()
 
     for ref, sent in (
-        (g_all.at[:, pl.ds(0, NX - 1)], "g"), (psend, "x"), (b1s, "b1"), (b2s, "b2"), (b3s, "b3"),
+        (g_all.at[:, pl.ds(0, NX - 1)], "g"), (psend, "x"), (b1s, "b1"), (b3s, "b3"),
         (sc.at[c, :, pl.ds(0, NZ - 1)], "c"), (sc.at[c], "p"), (d1s, "d1"), (d2s, "d2"),
     ):
         all_sent(ref, sent)
@@ -275,10 +294,8 @@
             vmem((NZ,), unit),
             vmem((NZ,), unit),
             vmem((NZ,), unit, F32),
-            vmem((9,), unit),
-            vmem((9,), unit),
-            vmem((2,), unit),
-            vmem((2,), unit),
+            vmem((11,), unit),
+            vmem((11,), unit),
             vmem((4,), unit),
             vmem((4,), unit),
             pltpu.VMEM((CORES, CHUNKS, NZ, *unit), BF16),
@@ -290,6 +307,7 @@
             pltpu.SemaphoreType.DMA((3,)),
             pltpu.SemaphoreType.DMA((len(SENT),)),
             pltpu.SemaphoreType.DMA((CHUNKS * len(ARRIVE),)),
+            pltpu.SemaphoreType.REGULAR((3,)),
         ],
         compiler_params=pltpu.CompilerParams(
             collective_id=0, has_side_effects=True, vmem_limit_bytes=67043328

time: 104 us -> 101 us (0.971)
  Pallas kernels: 102 us -> 99.3 us
    pallas_call x1, Pallas kernels: 102 us -> 99.3 us  [on_device(): pl.pallas_call(kernel, out_shape=jax.ShapeDtypeStruct((rows, depth), BF16...]
where the time goes in v4:
time: 101 us
  Pallas kernels  99.3 us (98%)
  local copies, waits for them, and re-layouts  1.53 us (2%)
    pallas_call x1, Pallas kernels, on_device(): pl.pallas_call(kernel, out_shape=jax.ShapeDtypeStruct((rows, depth), BF16...  99.3 us

profile of v4, /device:TPU:80, one launch (start us, length us, event | category | flops | bytes accessed | tf_op | source)
XLA Modules:
  0.0 100.9 jit_solution(11263821029004094416)
XLA Ops:
  0.0 99.3 %shard_map.37 = bf16[48,864]{1,0:T(8,128)(2,1)} custom-call(bf16[48,864]{1,0:T(8,128)(2,1)} %grad.1, bf16[864,1792]{1,0:T(8,128)(2,1)} %eig.1, bf16[384,1792]{1,0:T(8,128)(2,1)} %values.1), custom_call_target="tpu_custom_call" | custom-call | tf_op jit(solution)/shard_map/pallas_call | solution.py:285
  99.4 1.5 %copy.5 = bf16[48,864]{1,0:T(8,128)(2,1)} copy(bf16[48,864]{1,0:T(8,128)(2,1)} %shard_map.37) | data formatting | bytes 165888

commit v5 on v4

--- a/solution.py
+++ b/solution.py
@@ -28,9 +28,9 @@
     (2, "m1_sum"), (1, "meet_far"), (0, "meet_near"), (1, "meet_near"), (2, "meet_far"),
     (2, "meet_near"), (0, "final"), (1, "final"), (2, "final"), (0, "c_near"),
     (0, "c_far"), (1, "c_near"), (1, "c_far"), (2, "c_near"), (2, "c_far"),
-    (0, "c_end"), (0, "m2"), (1, "c_end"), (2, "c_end"), (1, "m2"),
-    (2, "m2"), (0, "d2"), (1, "d2"), (2, "d2"), (0, "df"),
-    (1, "df"), (2, "df"),
+    (0, "c_end"), (0, "m2"), (1, "c_end"), (0, "m2_sum"), (1, "m2"),
+    (1, "m2_sum"), (2, "c_end"), (2, "m2"), (2, "m2_sum"), (0, "d2"),
+    (1, "d2"), (2, "d2"), (0, "df"), (1, "df"), (2, "df"),
 )
 
 
@@ -231,9 +231,12 @@
 
         def m2():
             p = by_columns(sc[c, k].reshape(NZ * unit_rows, half), own_cols)
+            res[k] = p.reshape(res.shape[1:])
+
+        def m2_sum():
             arrived(k, sc.at[other, k], "p")
-            p = p + by_columns(sc[other, k].reshape(NZ * unit_rows, half), other_cols)
-            res[k] = p.reshape(res.shape[1:])
+            p = by_columns(sc[other, k].reshape(NZ * unit_rows, half), other_cols)
+            res[k] = res[k] + p.reshape(res.shape[1:])
             for slot, o, to in ((0, -4, -2), (1, -3, -1), (2, 3, 1)):
                 d1s[k, slot] = res[k, xx(o)].astype(BF16)
                 send(k, d1s.at[k, slot], d1r.at[k, slot], "d1", "d1", r, xx(to))
@@ -257,7 +260,7 @@
                 total = total + d2r[k, slot].astype(F32)
             out[pl.ds(k * h, h)] = total.astype(BF16)
 
-        steps = (a0, a_pass, m1, m1_sum, meet_far, meet_near, final, c_near, c_far, c_end, m2, d2, df)
+        steps = (a0, a_pass, m1, m1_sum, meet_far, meet_near, final, c_near, c_far, c_end, m2, m2_sum, d2, df)
         return {step.__name__: step for step in steps}
 
     chunks = {k: steps_of(k) for k in range(CHUNKS)}

time: 101 us -> 100 us (0.990)
  Pallas kernels: 99.3 us -> 97.9 us
    pallas_call x1, Pallas kernels: 99.3 us -> 97.9 us  [on_device(): pl.pallas_call(kernel, out_shape=jax.ShapeDtypeStruct((rows, depth), BF16...]
where the time goes in v5:
time: 100 us; the launch traced here: 99.5 us
  Pallas kernels  97.9 us (98%)
  local copies, waits for them, and re-layouts  1.53 us (2%)
    pallas_call x1, Pallas kernels, on_device(): pl.pallas_call(kernel, out_shape=jax.ShapeDtypeStruct((rows, depth), BF16...  97.9 us

profile of v5, /device:TPU:80, one launch (start us, length us, event | category | flops | bytes accessed | tf_op | source)
XLA Modules:
  0.0 99.5 jit_solution(11437714514120703877)
XLA Ops:
  0.0 97.9 %shard_map.37 = bf16[48,864]{1,0:T(8,128)(2,1)} custom-call(bf16[48,864]{1,0:T(8,128)(2,1)} %grad.1, bf16[864,1792]{1,0:T(8,128)(2,1)} %eig.1, bf16[384,1792]{1,0:T(8,128)(2,1)} %values.1), custom_call_target="tpu_custom_call" | custom-call | tf_op jit(solution)/shard_map/pallas_call | solution.py:288
  97.9 1.5 %copy.5 = bf16[48,864]{1,0:T(8,128)(2,1)} copy(bf16[48,864]{1,0:T(8,128)(2,1)} %shard_map.37) | data formatting | bytes 165888
